TPU v7x, 32 devices: a whole 2x2x4 slice. The times are simulated.
32 devices in a mesh: dp: 4 (over x, core), pipe: 4 (over z), tensor: 2 (over y).
Axes of the slice: x: 2, y: 2, z: 4, core: 2. Of those that a mesh axis runs over, the one named last changes fastest.
Arguments:
- support_tokens: int32 [32, 32], P(('dp', 'pipe')), may hold values from 0 to 64127
- support_lengths: int32 [32], P(('dp', 'pipe')), may hold values from 1 to 32
- support_labels: int32 [32, 1], P(('dp', 'pipe')), may hold values from 0 to 31
- query_tokens: int32 [16, 32], P(('dp', 'pipe')), may hold values from 0 to 64127
- query_lengths: int32 [16], P(('dp', 'pipe')), may hold values from 1 to 32
- query_episodes: int32 [16], P(('dp', 'pipe')), may hold values from 0 to 1
- embedding: bfloat16 [64128, 4096], P(('dp', 'pipe'), 'tensor'), may hold values from -18 to 18
- attn_gain: float32 [4, 4096], P('pipe'), may hold values from 0.5 to 1.5
- query_weight: bfloat16 [4, 4096, 4096], P('pipe', None, 'tensor'), may hold values from -1 to 1
- key_weight: bfloat16 [4, 4096, 1024], P('pipe', None, 'tensor'), may hold values from -16 to 16
- value_weight: bfloat16 [4, 4096, 1024], P('pipe', None, 'tensor'), may hold values from -0.09375 to 0.09375
- out_weight: bfloat16 [4, 4096, 4096], P('pipe', 'tensor'), may hold values from -0.09375 to 0.09375
- final_gain: float32 [4096], replicated, may hold values from 0.5 to 1.5
Outputs:
- prototypes: float32 [32, 4096], P(None, 'tensor')
- logits: float32 [16, 16], P(('dp', 'pipe'))
Inputs may be any that keep to these rules, and one draw needn't show every extreme that they name: `support_labels`: every class is the label of at least one support sequence.
All inputs are finite; a program needn't handle non-finite values.
Results may differ from a plain program's by a relative error of at most 0.024.
Values may be sent and summed in bfloat16 or wider, within the bound.
No kernel may reach another device: no remote copies, remote signals or barrier semaphores. Data moves between devices by JAX's collectives and lax.ppermute only.
A program may use at most 128 MiB of HBM per device.

v0:
```python
import math
import jax
import jax.numpy as jnp
from jax import lax
from jax.sharding import PartitionSpec as P

D = 4096
HEAD_DIM = 128
WAYS = 16
EPISODES = 2
epsilon = 1e-05
rotary_base = 500000.0


def passed_along(block, axis, distance):
    devices = range(lax.axis_size(axis))
    route = [((i - distance) % len(devices), i) for i in devices]
    return lax.ppermute(block, axis, route)


def rotate(heads_in, seq_len):
    half_dim = HEAD_DIM // 2
    freqs = jnp.exp(
        -math.log(rotary_base) * jnp.arange(half_dim, dtype=jnp.float32) * (2.0 / HEAD_DIM)
    )
    angles = jnp.arange(seq_len, dtype=jnp.float32)[:, None] * freqs[None, :]
    cosine = jnp.cos(angles)[None, :, None, :]
    sine = jnp.sin(angles)[None, :, None, :]
    first_half = heads_in[..., :half_dim]
    second_half = heads_in[..., half_dim:]
    return jnp.concatenate(
        [first_half * cosine - second_half * sine, second_half * cosine + first_half * sine],
        axis=-1,
    )


def whole_rows(hidden):
    return lax.all_gather(hidden, "tensor", axis=1, tiled=True)


def whole_values(full_rows, gain_vector):
    values = full_rows.astype(jnp.float32)
    mean_square = jnp.mean(values * values, axis=-1, keepdims=True)
    return values * lax.rsqrt(mean_square + epsilon) * gain_vector


def shards(
    support_tokens,
    support_lengths,
    support_labels,
    query_tokens,
    query_lengths,
    query_episodes,
    embedding,
    attn_gain,
    query_weight,
    key_weight,
    value_weight,
    out_weight,
    final_gain,
):
    group_count = lax.axis_size(("dp", "pipe"))
    sections = lax.axis_size("pipe")
    sup_dev, seq_len = support_tokens.shape
    qry_dev = query_tokens.shape[0]
    seq_count = sup_dev + qry_dev
    row_count = seq_count * seq_len
    table_rows, width = embedding.shape
    column_start = lax.axis_index("tensor") * width
    all_support, all_query, every_sup_len, every_qry_len = (
        lax.all_gather(support_tokens, ("dp", "pipe"), axis=0, tiled=True),
        lax.all_gather(query_tokens, ("dp", "pipe"), axis=0, tiled=True),
        lax.all_gather(support_lengths, ("dp", "pipe"), axis=0, tiled=True),
        lax.all_gather(query_lengths, ("dp", "pipe"), axis=0, tiled=True),
    )
    token_flat = jnp.concatenate(
        [all_support.reshape(group_count, sup_dev * seq_len), all_query], axis=1
    ).reshape(group_count * row_count)
    local_ids = token_flat - lax.axis_index(("dp", "pipe")) * table_rows
    inside = (local_ids >= 0) & (local_ids < table_rows)
    picked = jnp.take(embedding, jnp.clip(local_ids, 0, table_rows - 1), axis=0)
    picked = jnp.where(inside[:, None], picked, jnp.zeros_like(picked))
    hidden = lax.psum_scatter(
        picked.astype(jnp.float32).astype(jnp.bfloat16),
        ("dp", "pipe"),
        scatter_dimension=0,
        tiled=True,
    )
    seq_lengths = jnp.concatenate([support_lengths, query_lengths], axis=0)
    query_proj = query_weight[0]
    key_proj = key_weight[0]
    value_proj = value_weight[0]
    out_proj = out_weight[0]
    gain_vector = attn_gain[0]
    local_heads = query_proj.shape[1] // HEAD_DIM
    local_groups = key_proj.shape[1] // HEAD_DIM
    group_size = local_heads // local_groups
    w_in = jnp.concatenate([query_proj, key_proj, value_proj], axis=1)
    query_cols = local_heads * HEAD_DIM
    key_cols = local_groups * HEAD_DIM
    positions = jnp.arange(seq_len)
    causal = positions[None, :] <= positions[:, None]

    def section_block(stream, lengths_here):
        normed = whole_values(whole_rows(stream), gain_vector).astype(jnp.bfloat16)
        projected = jnp.dot(normed, w_in, preferred_element_type=jnp.float32)
        query_heads = projected[:, :query_cols].reshape(seq_count, seq_len, local_heads, HEAD_DIM)
        key_heads = projected[:, query_cols : query_cols + key_cols].reshape(
            seq_count, seq_len, local_groups, HEAD_DIM
        )
        value_heads = (
            projected[:, query_cols + key_cols :]
            .reshape(seq_count, seq_len, local_groups, HEAD_DIM)
            .astype(jnp.bfloat16)
        )
        query_heads = (
            rotate(query_heads, seq_len)
            .astype(jnp.bfloat16)
            .reshape(seq_count, seq_len, local_groups, group_size, HEAD_DIM)
        )
        key_heads = rotate(key_heads, seq_len).astype(jnp.bfloat16)
        scores = jnp.einsum(
            "sikgd,sjkd->skgij", query_heads, key_heads, preferred_element_type=jnp.float32
        ) / math.sqrt(HEAD_DIM)
        visible = causal[None, :, :] & (positions[None, None, :] < lengths_here[:, None, None])
        scores = jnp.where(visible[:, None, None, :, :], scores, -1e30)
        weights = jax.nn.softmax(scores, axis=-1).astype(jnp.bfloat16)
        mixed = jnp.einsum(
            "skgij,sjkd->sikgd", weights, value_heads, preferred_element_type=jnp.float32
        )
        mixed = mixed.astype(jnp.bfloat16).reshape(row_count, query_cols)
        partial_out = jnp.dot(mixed, out_proj, preferred_element_type=jnp.float32)
        summed = lax.psum_scatter(
            partial_out.astype(jnp.bfloat16), "tensor", scatter_dimension=1, tiled=True
        ).astype(jnp.float32)
        return (stream.astype(jnp.float32) + summed).astype(jnp.bfloat16)

    section_index = lax.axis_index("pipe")
    dp_base = lax.axis_index("dp") * sections

    def tick(tick_index, stream):
        held_group = dp_base + (section_index - tick_index) % sections
        sup_part = lax.dynamic_slice_in_dim(every_sup_len, held_group * sup_dev, sup_dev)
        qry_part = lax.dynamic_slice_in_dim(every_qry_len, held_group * qry_dev, qry_dev)
        lengths_here = jnp.concatenate([sup_part, qry_part], axis=0)
        first_tick = (tick_index - section_index) % sections
        active = (first_tick <= tick_index) & (tick_index < first_tick + sections)
        computed = section_block(stream, lengths_here)
        stream = jnp.where(active, computed, stream)
        return passed_along(stream, "pipe", 1)

    hidden = lax.fori_loop(0, 2 * sections, tick, hidden)
    final = lax.dynamic_slice_in_dim(
        whole_values(whole_rows(hidden), final_gain), column_start, width, 1
    )
    live = (positions[None, :] < seq_lengths[:, None]).astype(jnp.float32)
    pooled = jnp.sum(
        final.reshape(seq_count, seq_len, width) * live[:, :, None], axis=1
    ) / seq_lengths[:, None].astype(jnp.float32)
    support_pooled = pooled[:sup_dev]
    query_pooled = pooled[sup_dev:]
    class_count_all = EPISODES * WAYS
    onehot = (support_labels[:, 0][:, None] == jnp.arange(class_count_all)[None, :]).astype(
        jnp.float32
    )
    class_total = jnp.dot(onehot.T, support_pooled, precision=lax.Precision.HIGHEST)
    class_count = jnp.sum(onehot, axis=0)
    class_total, class_count = (
        lax.psum(class_total.astype(jnp.bfloat16), ("dp", "pipe")).astype(jnp.float32),
        lax.psum(class_count.astype(jnp.bfloat16), ("dp", "pipe")).astype(jnp.float32),
    )
    prototypes = class_total / class_count[:, None]
    episode_pick = (query_episodes[:, None] == jnp.arange(EPISODES)[None, :]).astype(jnp.float32)
    chosen = jnp.einsum(
        "qe,ewc->qwc",
        episode_pick,
        prototypes.reshape(EPISODES, WAYS, width),
        precision=lax.Precision.HIGHEST,
    )
    partial_distance = jnp.sum((query_pooled[:, None, :] - chosen) ** 2, axis=-1)
    distance = lax.psum(partial_distance, "tensor")
    logits = -distance / math.sqrt(D)
    return (prototypes, logits)


def solution(mesh):
    return jax.shard_map(
        shards,
        mesh=mesh,
        in_specs=(
            P(("dp", "pipe"), None),
            P(("dp", "pipe")),
            P(("dp", "pipe"), None),
            P(("dp", "pipe"), None),
            P(("dp", "pipe")),
            P(("dp", "pipe")),
            P(("dp", "pipe"), "tensor"),
            P("pipe", None),
            P("pipe", None, "tensor"),
            P("pipe", None, "tensor"),
            P("pipe", None, "tensor"),
            P("pipe", "tensor", None),
            P(),
        ),
        out_specs=(P(None, "tensor"), P(("dp", "pipe"), None)),
        check_vma=False,
    )
```

profile of v0, /device:TPU:8, one launch (start us, length us, event | category | flops | bytes accessed | tf_op | source)
XLA Modules:
  0.0 830.7 jit_solution(18302538500788156600)
XLA Ops:
  7.2 29.0 %all-gather.1 = s32[16,1,32]{2,1,0:T(1,128)S(1)} all-gather(s32[1,1,32]{2,1,0:T(1,128)} %bitcast.117), channel_id=1, replica_groups=mesh['dp'=4,'pipe'=4,'tensor'=2] {'dp','pipe'}, dimensions={0}, use_global_device_ids=true | all-gather | bytes 2176 | tf_op jit(solution)/shard_map/all_gather | solution.py:72
  36.2 33.0 %all-gather = s32[16,2,32]{2,1,0:T(2,128)S(1)} all-gather(s32[1,2,32]{2,1,0:T(2,128)} %bitcast.113), channel_id=1, replica_groups=mesh['dp'=4,'pipe'=4,'tensor'=2] {'dp','pipe'}, dimensions={0}, use_global_device_ids=true | all-gather | bytes 4352 | tf_op jit(solution)/shard_map/all_gather | solution.py:71
  69.7 20.5 %gather_fusion = bf16[1536,2048]{1,0:T(8,128)(2,1)} fusion(bf16[4008,2048]{1,0:T(8,128)(2,1)} %param.21, s32[2048]{0:T(1024)S(1)} %pad_clamp_fusion), kind=kCustom, calls=%fused_computation | custom fusion | bytes 12589056 | tf_op jit(solution)/shard_map/jit(_take)/gather | solution.py:81
  108.2 18.7 %pad_maximum_fusion = bf16[4096,3072]{1,0:T(8,128)(2,1)} fusion(bf16[4096,512]{1,0:T(8,128)(2,1)} %bitcast.104, bf16[4096,512]{1,0:T(8,128)(2,1)} %bitcast.105, bf16[4096,2048]{1,0:T(8,128)(2,1)} %bitcast.99), kind=kLoop, calls=%fused_computation.54 | loop fusion | flops 75497472 | bytes 50331648 | tf_op jit(solution)/shard_map/concatenate | solution.py:98
  126.8 53.5 %reduce-scatter.3.cloned.1.call-done = bf16[96,2048]{1,0:T(8,128)(2,1)} async-done(((bf16[1536,2048]{1,0:T(8,128)(2,1)}), bf16[96,2048]{1,0:T(8,128)(2,1)}) %reduce-scatter.3.cloned.1.call-update) | async-done | bytes 393232 | tf_op jit(solution)/shard_map/reduce_scatter | solution.py:83
  180.3 532.5 %while.16 = (s32[]{:T(128)}, bf16[96,2048]{1,0:T(8,128)(2,1)}, s32[]{:T(128)}, f32[1,4096]{1,0:T(1,128)S(1)}, bf16[4096,3072]{1,0:T(8,128)(2,1)}, /*index=5*/s32...) while((s32[]{:T(128)}, bf16[96,2048]{1,0:T(8,128)(2,1)}, ...), condition=%wide.region_6.7_spmd.clone, body=%wide.region_1.0_spmd.clone.sunk | while | flops 4072005120 | bytes 66611072 | solution.py:152
  180.4 11.0 %all_gather.32 = bf16[96,4096]{1,0:T(8,128)(2,1)S(1)} all-gather(bf16[96,2048]{1,0:T(8,128)(2,1)} %get-tuple-element.408), channel_id=1, replica_groups=mesh['dp'=4,'pipe'=4,'tensor'=2] {'tensor'}, dimensions={1}, use_global_device_ids=true | all-gather | bytes 1179648 | tf_op jit(solution)/shard_map/while/body/eval_jaxpr/all_gather | solution.py:38
  191.6 10.4 %fusion.89 = f32[96,3072]{1,0:T(8,128)S(1)} fusion(bf16[4096,3072]{1,0:T(8,128)(2,1)} %get-tuple-element.427, bf16[96,4096]{1,0:T(8,128)(2,1)S(1)} %all_gather.32, f32[4096]{0:T(1024)S(1)} %bitcast.108, f32[96]{0:T(128)S(1)} %add_rsqrt_fusion.3), kind=kOutput, calls=%fused_computation.17.clone.1 | convolution fusion | flops 2417491968 | bytes 27148672 | tf_op jit(solution)/shard_map/while/body/eval_jaxpr/dot_general | solution.py:106
  207.3 9.5 %convolution_convert_fusion.4 = bf16[96,4096]{1,0:T(8,128)(2,1)} fusion(bf16[96,2048]{1,0:T(8,128)(2,1)S(1)} %reshape.325, bf16[2048,4096]{1,0:T(8,128)(2,1)} %get-tuple-element.431), kind=kOutput, calls=%fused_computation.4.clone.1 | convolution fusion | flops 1611005952 | bytes 17956864 | tf_op jit(solution)/shard_map/while/body/eval_jaxpr/dot_general | solution.py:132
  216.9 17.6 %reduce-scatter.5.cloned.1.call-done = bf16[96,2048]{1,0:T(8,128)(2,1)} async-done(((bf16[96,4096]{1,0:T(8,128)(2,1)}), bf16[96,2048]{1,0:T(8,128)(2,1)}) %reduce-scatter.5.cloned.1.call-update) | async-done | bytes 393232 | tf_op jit(solution)/shard_map/while/body/eval_jaxpr/reduce_scatter | solution.py:133
  237.1 9.2 %collective-permute-done = bf16[96,2048]{1,0:T(8,128)(2,1)S(1)} collective-permute-done((bf16[96,2048]{1,0:T(8,128)(2,1)S(1)}, bf16[96,2048]{1,0:T(8,128)(2,1)S(1)}, u32[]{:S(2)}, u32[]{:S(2)}) %collective-permute-start) | collective-permute-done | bytes 393248 | tf_op jit(solution)/shard_map/while/body/eval_jaxpr/ppermute | solution.py:18
  247.2 10.7 %all_gather.32 = bf16[96,4096]{1,0:T(8,128)(2,1)S(1)} all-gather(bf16[96,2048]{1,0:T(8,128)(2,1)} %get-tuple-element.408), channel_id=1, replica_groups=mesh['dp'=4,'pipe'=4,'tensor'=2] {'tensor'}, dimensions={1}, use_global_device_ids=true | all-gather | bytes 1179648 | tf_op jit(solution)/shard_map/while/body/eval_jaxpr/all_gather | solution.py:38
  258.1 10.4 %fusion.89 = f32[96,3072]{1,0:T(8,128)S(1)} fusion(bf16[4096,3072]{1,0:T(8,128)(2,1)} %get-tuple-element.427, bf16[96,4096]{1,0:T(8,128)(2,1)S(1)} %all_gather.32, f32[4096]{0:T(1024)S(1)} %bitcast.108, f32[96]{0:T(128)S(1)} %add_rsqrt_fusion.3), kind=kOutput, calls=%fused_computation.17.clone.1 | convolution fusion | flops 2417491968 | bytes 27148672 | tf_op jit(solution)/shard_map/while/body/eval_jaxpr/dot_general | solution.py:106
  273.8 9.5 %convolution_convert_fusion.4 = bf16[96,4096]{1,0:T(8,128)(2,1)} fusion(bf16[96,2048]{1,0:T(8,128)(2,1)S(1)} %reshape.325, bf16[2048,4096]{1,0:T(8,128)(2,1)} %get-tuple-element.431), kind=kOutput, calls=%fused_computation.4.clone.1 | convolution fusion | flops 1611005952 | bytes 17956864 | tf_op jit(solution)/shard_map/while/body/eval_jaxpr/dot_general | solution.py:132
  283.4 17.6 %reduce-scatter.5.cloned.1.call-done = bf16[96,2048]{1,0:T(8,128)(2,1)} async-done(((bf16[96,4096]{1,0:T(8,128)(2,1)}), bf16[96,2048]{1,0:T(8,128)(2,1)}) %reduce-scatter.5.cloned.1.call-update) | async-done | bytes 393232 | tf_op jit(solution)/shard_map/while/body/eval_jaxpr/reduce_scatter | solution.py:133
  303.7 9.2 %collective-permute-done = bf16[96,2048]{1,0:T(8,128)(2,1)S(1)} collective-permute-done((bf16[96,2048]{1,0:T(8,128)(2,1)S(1)}, bf16[96,2048]{1,0:T(8,128)(2,1)S(1)}, u32[]{:S(2)}, u32[]{:S(2)}) %collective-permute-start) | collective-permute-done | bytes 393248 | tf_op jit(solution)/shard_map/while/body/eval_jaxpr/ppermute | solution.py:18
  313.7 10.7 %all_gather.32 = bf16[96,4096]{1,0:T(8,128)(2,1)S(1)} all-gather(bf16[96,2048]{1,0:T(8,128)(2,1)} %get-tuple-element.408), channel_id=1, replica_groups=mesh['dp'=4,'pipe'=4,'tensor'=2] {'tensor'}, dimensions={1}, use_global_device_ids=true | all-gather | bytes 1179648 | tf_op jit(solution)/shard_map/while/body/eval_jaxpr/all_gather | solution.py:38
  324.6 10.4 %fusion.89 = f32[96,3072]{1,0:T(8,128)S(1)} fusion(bf16[4096,3072]{1,0:T(8,128)(2,1)} %get-tuple-element.427, bf16[96,4096]{1,0:T(8,128)(2,1)S(1)} %all_gather.32, f32[4096]{0:T(1024)S(1)} %bitcast.108, f32[96]{0:T(128)S(1)} %add_rsqrt_fusion.3), kind=kOutput, calls=%fused_computation.17.clone.1 | convolution fusion | flops 2417491968 | bytes 27148672 | tf_op jit(solution)/shard_map/while/body/eval_jaxpr/dot_general | solution.py:106
  340.3 9.5 %convolution_convert_fusion.4 = bf16[96,4096]{1,0:T(8,128)(2,1)} fusion(bf16[96,2048]{1,0:T(8,128)(2,1)S(1)} %reshape.325, bf16[2048,4096]{1,0:T(8,128)(2,1)} %get-tuple-element.431), kind=kOutput, calls=%fused_computation.4.clone.1 | convolution fusion | flops 1611005952 | bytes 17956864 | tf_op jit(solution)/shard_map/while/body/eval_jaxpr/dot_general | solution.py:132
  349.9 17.7 %reduce-scatter.5.cloned.1.call-done = bf16[96,2048]{1,0:T(8,128)(2,1)} async-done(((bf16[96,4096]{1,0:T(8,128)(2,1)}), bf16[96,2048]{1,0:T(8,128)(2,1)}) %reduce-scatter.5.cloned.1.call-update) | async-done | bytes 393232 | tf_op jit(solution)/shard_map/while/body/eval_jaxpr/reduce_scatter | solution.py:133
  380.2 10.7 %all_gather.32 = bf16[96,4096]{1,0:T(8,128)(2,1)S(1)} all-gather(bf16[96,2048]{1,0:T(8,128)(2,1)} %get-tuple-element.408), channel_id=1, replica_groups=mesh['dp'=4,'pipe'=4,'tensor'=2] {'tensor'}, dimensions={1}, use_global_device_ids=true | all-gather | bytes 1179648 | tf_op jit(solution)/shard_map/while/body/eval_jaxpr/all_gather | solution.py:38
  391.2 10.4 %fusion.89 = f32[96,3072]{1,0:T(8,128)S(1)} fusion(bf16[4096,3072]{1,0:T(8,128)(2,1)} %get-tuple-element.427, bf16[96,4096]{1,0:T(8,128)(2,1)S(1)} %all_gather.32, f32[4096]{0:T(1024)S(1)} %bitcast.108, f32[96]{0:T(128)S(1)} %add_rsqrt_fusion.3), kind=kOutput, calls=%fused_computation.17.clone.1 | convolution fusion | flops 2417491968 | bytes 27148672 | tf_op jit(solution)/shard_map/while/body/eval_jaxpr/dot_general | solution.py:106
  406.8 9.5 %convolution_convert_fusion.4 = bf16[96,4096]{1,0:T(8,128)(2,1)} fusion(bf16[96,2048]{1,0:T(8,128)(2,1)S(1)} %reshape.325, bf16[2048,4096]{1,0:T(8,128)(2,1)} %get-tuple-element.431), kind=kOutput, calls=%fused_computation.4.clone.1 | convolution fusion | flops 1611005952 | bytes 17956864 | tf_op jit(solution)/shard_map/while/body/eval_jaxpr/dot_general | solution.py:132
  416.4 17.6 %reduce-scatter.5.cloned.1.call-done = bf16[96,2048]{1,0:T(8,128)(2,1)} async-done(((bf16[96,4096]{1,0:T(8,128)(2,1)}), bf16[96,2048]{1,0:T(8,128)(2,1)}) %reduce-scatter.5.cloned.1.call-update) | async-done | bytes 393232 | tf_op jit(solution)/shard_map/while/body/eval_jaxpr/reduce_scatter | solution.py:133
  436.7 9.2 %collective-permute-done = bf16[96,2048]{1,0:T(8,128)(2,1)S(1)} collective-permute-done((bf16[96,2048]{1,0:T(8,128)(2,1)S(1)}, bf16[96,2048]{1,0:T(8,128)(2,1)S(1)}, u32[]{:S(2)}, u32[]{:S(2)}) %collective-permute-start) | collective-permute-done | bytes 393248 | tf_op jit(solution)/shard_map/while/body/eval_jaxpr/ppermute | solution.py:18
  446.7 10.7 %all_gather.32 = bf16[96,4096]{1,0:T(8,128)(2,1)S(1)} all-gather(bf16[96,2048]{1,0:T(8,128)(2,1)} %get-tuple-element.408), channel_id=1, replica_groups=mesh['dp'=4,'pipe'=4,'tensor'=2] {'tensor'}, dimensions={1}, use_global_device_ids=true | all-gather | bytes 1179648 | tf_op jit(solution)/shard_map/while/body/eval_jaxpr/all_gather | solution.py:38
  457.7 10.4 %fusion.89 = f32[96,3072]{1,0:T(8,128)S(1)} fusion(bf16[4096,3072]{1,0:T(8,128)(2,1)} %get-tuple-element.427, bf16[96,4096]{1,0:T(8,128)(2,1)S(1)} %all_gather.32, f32[4096]{0:T(1024)S(1)} %bitcast.108, f32[96]{0:T(128)S(1)} %add_rsqrt_fusion.3), kind=kOutput, calls=%fused_computation.17.clone.1 | convolution fusion | flops 2417491968 | bytes 27148672 | tf_op jit(solution)/shard_map/while/body/eval_jaxpr/dot_general | solution.py:106
  473.4 9.5 %convolution_convert_fusion.4 = bf16[96,4096]{1,0:T(8,128)(2,1)} fusion(bf16[96,2048]{1,0:T(8,128)(2,1)S(1)} %reshape.325, bf16[2048,4096]{1,0:T(8,128)(2,1)} %get-tuple-element.431), kind=kOutput, calls=%fused_computation.4.clone.1 | convolution fusion | flops 1611005952 | bytes 17956864 | tf_op jit(solution)/shard_map/while/body/eval_jaxpr/dot_general | solution.py:132
  483.0 17.6 %reduce-scatter.5.cloned.1.call-done = bf16[96,2048]{1,0:T(8,128)(2,1)} async-done(((bf16[96,4096]{1,0:T(8,128)(2,1)}), bf16[96,2048]{1,0:T(8,128)(2,1)}) %reduce-scatter.5.cloned.1.call-update) | async-done | bytes 393232 | tf_op jit(solution)/shard_map/while/body/eval_jaxpr/reduce_scatter | solution.py:133
  503.3 9.2 %collective-permute-done = bf16[96,2048]{1,0:T(8,128)(2,1)S(1)} collective-permute-done((bf16[96,2048]{1,0:T(8,128)(2,1)S(1)}, bf16[96,2048]{1,0:T(8,128)(2,1)S(1)}, u32[]{:S(2)}, u32[]{:S(2)}) %collective-permute-start) | collective-permute-done | bytes 393248 | tf_op jit(solution)/shard_map/while/body/eval_jaxpr/ppermute | solution.py:18
  513.3 10.7 %all_gather.32 = bf16[96,4096]{1,0:T(8,128)(2,1)S(1)} all-gather(bf16[96,2048]{1,0:T(8,128)(2,1)} %get-tuple-element.408), channel_id=1, replica_groups=mesh['dp'=4,'pipe'=4,'tensor'=2] {'tensor'}, dimensions={1}, use_global_device_ids=true | all-gather | bytes 1179648 | tf_op jit(solution)/shard_map/while/body/eval_jaxpr/all_gather | solution.py:38
  524.2 10.4 %fusion.89 = f32[96,3072]{1,0:T(8,128)S(1)} fusion(bf16[4096,3072]{1,0:T(8,128)(2,1)} %get-tuple-element.427, bf16[96,4096]{1,0:T(8,128)(2,1)S(1)} %all_gather.32, f32[4096]{0:T(1024)S(1)} %bitcast.108, f32[96]{0:T(128)S(1)} %add_rsqrt_fusion.3), kind=kOutput, calls=%fused_computation.17.clone.1 | convolution fusion | flops 2417491968 | bytes 27148672 | tf_op jit(solution)/shard_map/while/body/eval_jaxpr/dot_general | solution.py:106
  539.9 9.5 %convolution_convert_fusion.4 = bf16[96,4096]{1,0:T(8,128)(2,1)} fusion(bf16[96,2048]{1,0:T(8,128)(2,1)S(1)} %reshape.325, bf16[2048,4096]{1,0:T(8,128)(2,1)} %get-tuple-element.431), kind=kOutput, calls=%fused_computation.4.clone.1 | convolution fusion | flops 1611005952 | bytes 17956864 | tf_op jit(solution)/shard_map/while/body/eval_jaxpr/dot_general | solution.py:132
  549.5 17.6 %reduce-scatter.5.cloned.1.call-done = bf16[96,2048]{1,0:T(8,128)(2,1)} async-done(((bf16[96,4096]{1,0:T(8,128)(2,1)}), bf16[96,2048]{1,0:T(8,128)(2,1)}) %reduce-scatter.5.cloned.1.call-update) | async-done | bytes 393232 | tf_op jit(solution)/shard_map/while/body/eval_jaxpr/reduce_scatter | solution.py:133
  569.8 9.2 %collective-permute-done = bf16[96,2048]{1,0:T(8,128)(2,1)S(1)} collective-permute-done((bf16[96,2048]{1,0:T(8,128)(2,1)S(1)}, bf16[96,2048]{1,0:T(8,128)(2,1)S(1)}, u32[]{:S(2)}, u32[]{:S(2)}) %collective-permute-start) | collective-permute-done | bytes 393248 | tf_op jit(solution)/shard_map/while/body/eval_jaxpr/ppermute | solution.py:18
  579.8 10.7 %all_gather.32 = bf16[96,4096]{1,0:T(8,128)(2,1)S(1)} all-gather(bf16[96,2048]{1,0:T(8,128)(2,1)} %get-tuple-element.408), channel_id=1, replica_groups=mesh['dp'=4,'pipe'=4,'tensor'=2] {'tensor'}, dimensions={1}, use_global_device_ids=true | all-gather | bytes 1179648 | tf_op jit(solution)/shard_map/while/body/eval_jaxpr/all_gather | solution.py:38
  590.8 10.4 %fusion.89 = f32[96,3072]{1,0:T(8,128)S(1)} fusion(bf16[4096,3072]{1,0:T(8,128)(2,1)} %get-tuple-element.427, bf16[96,4096]{1,0:T(8,128)(2,1)S(1)} %all_gather.32, f32[4096]{0:T(1024)S(1)} %bitcast.108, f32[96]{0:T(128)S(1)} %add_rsqrt_fusion.3), kind=kOutput, calls=%fused_computation.17.clone.1 | convolution fusion | flops 2417491968 | bytes 27148672 | tf_op jit(solution)/shard_map/while/body/eval_jaxpr/dot_general | solution.py:106
  606.5 9.5 %convolution_convert_fusion.4 = bf16[96,4096]{1,0:T(8,128)(2,1)} fusion(bf16[96,2048]{1,0:T(8,128)(2,1)S(1)} %reshape.325, bf16[2048,4096]{1,0:T(8,128)(2,1)} %get-tuple-element.431), kind=kOutput, calls=%fused_computation.4.clone.1 | convolution fusion | flops 1611005952 | bytes 17956864 | tf_op jit(solution)/shard_map/while/body/eval_jaxpr/dot_general | solution.py:132
  616.0 17.6 %reduce-scatter.5.cloned.1.call-done = bf16[96,2048]{1,0:T(8,128)(2,1)} async-done(((bf16[96,4096]{1,0:T(8,128)(2,1)}), bf16[96,2048]{1,0:T(8,128)(2,1)}) %reduce-scatter.5.cloned.1.call-update) | async-done | bytes 393232 | tf_op jit(solution)/shard_map/while/body/eval_jaxpr/reduce_scatter | solution.py:133
  636.3 9.2 %collective-permute-done = bf16[96,2048]{1,0:T(8,128)(2,1)S(1)} collective-permute-done((bf16[96,2048]{1,0:T(8,128)(2,1)S(1)}, bf16[96,2048]{1,0:T(8,128)(2,1)S(1)}, u32[]{:S(2)}, u32[]{:S(2)}) %collective-permute-start) | collective-permute-done | bytes 393248 | tf_op jit(solution)/shard_map/while/body/eval_jaxpr/ppermute | solution.py:18
  646.3 10.7 %all_gather.32 = bf16[96,4096]{1,0:T(8,128)(2,1)S(1)} all-gather(bf16[96,2048]{1,0:T(8,128)(2,1)} %get-tuple-element.408), channel_id=1, replica_groups=mesh['dp'=4,'pipe'=4,'tensor'=2] {'tensor'}, dimensions={1}, use_global_device_ids=true | all-gather | bytes 1179648 | tf_op jit(solution)/shard_map/while/body/eval_jaxpr/all_gather | solution.py:38
  657.3 10.4 %fusion.89 = f32[96,3072]{1,0:T(8,128)S(1)} fusion(bf16[4096,3072]{1,0:T(8,128)(2,1)} %get-tuple-element.427, bf16[96,4096]{1,0:T(8,128)(2,1)S(1)} %all_gather.32, f32[4096]{0:T(1024)S(1)} %bitcast.108, f32[96]{0:T(128)S(1)} %add_rsqrt_fusion.3), kind=kOutput, calls=%fused_computation.17.clone.1 | convolution fusion | flops 2417491968 | bytes 27148672 | tf_op jit(solution)/shard_map/while/body/eval_jaxpr/dot_general | solution.py:106
  673.0 9.5 %convolution_convert_fusion.4 = bf16[96,4096]{1,0:T(8,128)(2,1)} fusion(bf16[96,2048]{1,0:T(8,128)(2,1)S(1)} %reshape.325, bf16[2048,4096]{1,0:T(8,128)(2,1)} %get-tuple-element.431), kind=kOutput, calls=%fused_computation.4.clone.1 | convolution fusion | flops 1611005952 | bytes 17956864 | tf_op jit(solution)/shard_map/while/body/eval_jaxpr/dot_general | solution.py:132
  682.5 17.6 %reduce-scatter.5.cloned.1.call-done = bf16[96,2048]{1,0:T(8,128)(2,1)} async-done(((bf16[96,4096]{1,0:T(8,128)(2,1)}), bf16[96,2048]{1,0:T(8,128)(2,1)}) %reduce-scatter.5.cloned.1.call-update) | async-done | bytes 393232 | tf_op jit(solution)/shard_map/while/body/eval_jaxpr/reduce_scatter | solution.py:133
  702.8 9.2 %collective-permute-done = bf16[96,2048]{1,0:T(8,128)(2,1)S(1)} collective-permute-done((bf16[96,2048]{1,0:T(8,128)(2,1)S(1)}, bf16[96,2048]{1,0:T(8,128)(2,1)S(1)}, u32[]{:S(2)}, u32[]{:S(2)}) %collective-permute-start) | collective-permute-done | bytes 393248 | tf_op jit(solution)/shard_map/while/body/eval_jaxpr/ppermute | solution.py:18
  712.8 10.8 %all_gather.29 = bf16[96,4096]{1,0:T(8,128)(2,1)S(1)} all-gather(bf16[96,2048]{1,0:T(8,128)(2,1)} %get-tuple-element.268), channel_id=1, replica_groups=mesh['dp'=4,'pipe'=4,'tensor'=2] {'tensor'}, dimensions={1}, use_global_device_ids=true | all-gather | bytes 1179648 | tf_op jit(solution)/shard_map/all_gather | solution.py:38
  725.6 32.3 %psum.22 = bf16[32]{0:T(256)(128)(2,1)S(1)} all-reduce(bf16[32]{0:T(256)(128)(2,1)S(1)} %convert_reduce_fusion), channel_id=1, replica_groups=mesh['dp'=4,'pipe'=4,'tensor'=2] {'dp','pipe'}, use_global_device_ids=true, to_apply=%region_11.12 | all-reduce | flops 32 | bytes 128 | tf_op jit(solution)/shard_map/psum | solution.py:170
  758.6 57.9 %all-reduce.5.cloned.1.call-done = bf16[32,2048]{1,0:T(8,128)(2,1)} async-done(((bf16[32,2048]{1,0:T(8,128)(2,1)}), bf16[32,2048]{1,0:T(8,128)(2,1)}) %all-reduce.5.cloned.1.call-update) | async-done | bytes 131088 | tf_op jit(solution)/shard_map/psum | solution.py:169
  (314 shorter events, 106.5 us)
Async XLA Ops:
  7.2 173.2 %reduce-scatter.3.cloned.1.call-start = ((), (), s32[]{:S(2)}) async-start(), calls=%async_computation.2 | async-start | bytes 6684672 | tf_op jit(solution)/shard_map/reduce_scatter | solution.py:83
  97.3 0.7 copy-start.6
  97.3 2.1 copy-start.5
  108.2 72.1 %copy-start.2 = (f32[1,4096]{1,0:T(1,128)S(1)}, f32[1,4096]{1,0:T(1,128)}, u32[]{:S(2)}) copy-start(f32[1,4096]{1,0:T(1,128)} %param.22) | copy-start | bytes 49156
  180.3 543.7 %dynamic-slice-start = ((f32[4096]{0:T(1024)}, s32[]{:T(128)}), f32[2048]{0:T(1024)S(1)}, s32[]{:S(2)}) async-start(f32[4096]{0:T(1024)} %param.27, s32[]{:T(128)} %select_n.115), calls=%async_computation.5 | async-start | bytes 16896 | tf_op jit(solution)/shard_map/dynamic_slice | solution.py:153
  180.3 54.2 %reduce-scatter.5.cloned.1.call-start = ((), (), s32[]{:S(2)}) async-start(), calls=%async_computation.4 | async-start | bytes 1179648 | tf_op jit(solution)/shard_map/while/body/eval_jaxpr/reduce_scatter | solution.py:133
  207.3 27.2 %copy-start = (bf16[96,2048]{1,0:T(8,128)(2,1)S(1)}, bf16[96,2048]{1,0:T(8,128)(2,1)}, u32[]{:S(2)}) copy-start(bf16[96,2048]{1,0:T(8,128)(2,1)} %get-tuple-element.408) | copy-start | bytes 1179652 | tf_op jit(solution)/shard_map/while
  235.6 10.8 %collective-permute-start = (bf16[96,2048]{1,0:T(8,128)(2,1)S(1)}, bf16[96,2048]{1,0:T(8,128)(2,1)S(1)}, u32[]{:S(2)}, u32[]{:S(2)}) collective-permute-start(bf16[96,2048]{1,0:T(8,128)(2,1)S(1)} %fusion.94), channel_id=1, source_target_pairs={{6,0},{0,2},{2,4},{4,6},{7,1},{1,3},{3,5},{5,7},{14,8},{8,10},{10,... | collective-permute-start | bytes 1179656 | tf_op jit(solution)/shard_map/while/body/eval_jaxpr/ppermute | solution.py:18
  246.4 0.8 copy-start.1
  247.1 53.9 %reduce-scatter.5.cloned.1.call-start = ((), (), s32[]{:S(2)}) async-start(), calls=%async_computation.4 | async-start | bytes 1179648 | tf_op jit(solution)/shard_map/while/body/eval_jaxpr/reduce_scatter | solution.py:133
  273.8 27.2 %copy-start = (bf16[96,2048]{1,0:T(8,128)(2,1)S(1)}, bf16[96,2048]{1,0:T(8,128)(2,1)}, u32[]{:S(2)}) copy-start(bf16[96,2048]{1,0:T(8,128)(2,1)} %get-tuple-element.408) | copy-start | bytes 1179652 | tf_op jit(solution)/shard_map/while
  302.1 10.7 %collective-permute-start = (bf16[96,2048]{1,0:T(8,128)(2,1)S(1)}, bf16[96,2048]{1,0:T(8,128)(2,1)S(1)}, u32[]{:S(2)}, u32[]{:S(2)}) collective-permute-start(bf16[96,2048]{1,0:T(8,128)(2,1)S(1)} %fusion.94), channel_id=1, source_target_pairs={{6,0},{0,2},{2,4},{4,6},{7,1},{1,3},{3,5},{5,7},{14,8},{8,10},{10,... | collective-permute-start | bytes 1179656 | tf_op jit(solution)/shard_map/while/body/eval_jaxpr/ppermute | solution.py:18
  312.9 0.8 copy-start.1
  313.6 53.9 %reduce-scatter.5.cloned.1.call-start = ((), (), s32[]{:S(2)}) async-start(), calls=%async_computation.4 | async-start | bytes 1179648 | tf_op jit(solution)/shard_map/while/body/eval_jaxpr/reduce_scatter | solution.py:133
  340.3 27.3 %copy-start = (bf16[96,2048]{1,0:T(8,128)(2,1)S(1)}, bf16[96,2048]{1,0:T(8,128)(2,1)}, u32[]{:S(2)}) copy-start(bf16[96,2048]{1,0:T(8,128)(2,1)} %get-tuple-element.408) | copy-start | bytes 1179652 | tf_op jit(solution)/shard_map/while
  368.7 10.7 %collective-permute-start = (bf16[96,2048]{1,0:T(8,128)(2,1)S(1)}, bf16[96,2048]{1,0:T(8,128)(2,1)S(1)}, u32[]{:S(2)}, u32[]{:S(2)}) collective-permute-start(bf16[96,2048]{1,0:T(8,128)(2,1)S(1)} %fusion.94), channel_id=1, source_target_pairs={{6,0},{0,2},{2,4},{4,6},{7,1},{1,3},{3,5},{5,7},{14,8},{8,10},{10,... | collective-permute-start | bytes 1179656 | tf_op jit(solution)/shard_map/while/body/eval_jaxpr/ppermute | solution.py:18
  379.4 0.8 copy-start.1
  380.2 53.9 %reduce-scatter.5.cloned.1.call-start = ((), (), s32[]{:S(2)}) async-start(), calls=%async_computation.4 | async-start | bytes 1179648 | tf_op jit(solution)/shard_map/while/body/eval_jaxpr/reduce_scatter | solution.py:133
  406.8 27.2 %copy-start = (bf16[96,2048]{1,0:T(8,128)(2,1)S(1)}, bf16[96,2048]{1,0:T(8,128)(2,1)}, u32[]{:S(2)}) copy-start(bf16[96,2048]{1,0:T(8,128)(2,1)} %get-tuple-element.408) | copy-start | bytes 1179652 | tf_op jit(solution)/shard_map/while
  435.2 10.8 %collective-permute-start = (bf16[96,2048]{1,0:T(8,128)(2,1)S(1)}, bf16[96,2048]{1,0:T(8,128)(2,1)S(1)}, u32[]{:S(2)}, u32[]{:S(2)}) collective-permute-start(bf16[96,2048]{1,0:T(8,128)(2,1)S(1)} %fusion.94), channel_id=1, source_target_pairs={{6,0},{0,2},{2,4},{4,6},{7,1},{1,3},{3,5},{5,7},{14,8},{8,10},{10,... | collective-permute-start | bytes 1179656 | tf_op jit(solution)/shard_map/while/body/eval_jaxpr/ppermute | solution.py:18
  445.9 0.8 copy-start.1
  446.7 53.9 %reduce-scatter.5.cloned.1.call-start = ((), (), s32[]{:S(2)}) async-start(), calls=%async_computation.4 | async-start | bytes 1179648 | tf_op jit(solution)/shard_map/while/body/eval_jaxpr/reduce_scatter | solution.py:133
  473.4 27.2 %copy-start = (bf16[96,2048]{1,0:T(8,128)(2,1)S(1)}, bf16[96,2048]{1,0:T(8,128)(2,1)}, u32[]{:S(2)}) copy-start(bf16[96,2048]{1,0:T(8,128)(2,1)} %get-tuple-element.408) | copy-start | bytes 1179652 | tf_op jit(solution)/shard_map/while
  501.7 10.7 %collective-permute-start = (bf16[96,2048]{1,0:T(8,128)(2,1)S(1)}, bf16[96,2048]{1,0:T(8,128)(2,1)S(1)}, u32[]{:S(2)}, u32[]{:S(2)}) collective-permute-start(bf16[96,2048]{1,0:T(8,128)(2,1)S(1)} %fusion.94), channel_id=1, source_target_pairs={{6,0},{0,2},{2,4},{4,6},{7,1},{1,3},{3,5},{5,7},{14,8},{8,10},{10,... | collective-permute-start | bytes 1179656 | tf_op jit(solution)/shard_map/while/body/eval_jaxpr/ppermute | solution.py:18
  512.5 0.8 copy-start.1
  513.2 53.9 %reduce-scatter.5.cloned.1.call-start = ((), (), s32[]{:S(2)}) async-start(), calls=%async_computation.4 | async-start | bytes 1179648 | tf_op jit(solution)/shard_map/while/body/eval_jaxpr/reduce_scatter | solution.py:133
  539.9 27.2 %copy-start = (bf16[96,2048]{1,0:T(8,128)(2,1)S(1)}, bf16[96,2048]{1,0:T(8,128)(2,1)}, u32[]{:S(2)}) copy-start(bf16[96,2048]{1,0:T(8,128)(2,1)} %get-tuple-element.408) | copy-start | bytes 1179652 | tf_op jit(solution)/shard_map/while
  568.2 10.8 %collective-permute-start = (bf16[96,2048]{1,0:T(8,128)(2,1)S(1)}, bf16[96,2048]{1,0:T(8,128)(2,1)S(1)}, u32[]{:S(2)}, u32[]{:S(2)}) collective-permute-start(bf16[96,2048]{1,0:T(8,128)(2,1)S(1)} %fusion.94), channel_id=1, source_target_pairs={{6,0},{0,2},{2,4},{4,6},{7,1},{1,3},{3,5},{5,7},{14,8},{8,10},{10,... | collective-permute-start | bytes 1179656 | tf_op jit(solution)/shard_map/while/body/eval_jaxpr/ppermute | solution.py:18
  579.0 0.8 copy-start.1
  579.8 53.8 %reduce-scatter.5.cloned.1.call-start = ((), (), s32[]{:S(2)}) async-start(), calls=%async_computation.4 | async-start | bytes 1179648 | tf_op jit(solution)/shard_map/while/body/eval_jaxpr/reduce_scatter | solution.py:133
  606.5 27.2 %copy-start = (bf16[96,2048]{1,0:T(8,128)(2,1)S(1)}, bf16[96,2048]{1,0:T(8,128)(2,1)}, u32[]{:S(2)}) copy-start(bf16[96,2048]{1,0:T(8,128)(2,1)} %get-tuple-element.408) | copy-start | bytes 1179652 | tf_op jit(solution)/shard_map/while
  634.8 10.8 %collective-permute-start = (bf16[96,2048]{1,0:T(8,128)(2,1)S(1)}, bf16[96,2048]{1,0:T(8,128)(2,1)S(1)}, u32[]{:S(2)}, u32[]{:S(2)}) collective-permute-start(bf16[96,2048]{1,0:T(8,128)(2,1)S(1)} %fusion.94), channel_id=1, source_target_pairs={{6,0},{0,2},{2,4},{4,6},{7,1},{1,3},{3,5},{5,7},{14,8},{8,10},{10,... | collective-permute-start | bytes 1179656 | tf_op jit(solution)/shard_map/while/body/eval_jaxpr/ppermute | solution.py:18
  645.5 0.8 copy-start.1
  646.3 53.9 %reduce-scatter.5.cloned.1.call-start = ((), (), s32[]{:S(2)}) async-start(), calls=%async_computation.4 | async-start | bytes 1179648 | tf_op jit(solution)/shard_map/while/body/eval_jaxpr/reduce_scatter | solution.py:133
  673.0 27.2 %copy-start = (bf16[96,2048]{1,0:T(8,128)(2,1)S(1)}, bf16[96,2048]{1,0:T(8,128)(2,1)}, u32[]{:S(2)}) copy-start(bf16[96,2048]{1,0:T(8,128)(2,1)} %get-tuple-element.408) | copy-start | bytes 1179652 | tf_op jit(solution)/shard_map/while
  701.3 10.7 %collective-permute-start = (bf16[96,2048]{1,0:T(8,128)(2,1)S(1)}, bf16[96,2048]{1,0:T(8,128)(2,1)S(1)}, u32[]{:S(2)}, u32[]{:S(2)}) collective-permute-start(bf16[96,2048]{1,0:T(8,128)(2,1)S(1)} %fusion.94), channel_id=1, source_target_pairs={{6,0},{0,2},{2,4},{4,6},{7,1},{1,3},{3,5},{5,7},{14,8},{8,10},{10,... | collective-permute-start | bytes 1179656 | tf_op jit(solution)/shard_map/while/body/eval_jaxpr/ppermute | solution.py:18
  712.0 0.8 copy-start.1
  712.8 11.6 %copy-start.4 = (s32[2,1]{0,1:T(1,128)S(1)}, s32[2,1]{0,1:T(1,128)}, u32[]{:S(2)}) copy-start(s32[2,1]{0,1:T(1,128)} %param.17) | copy-start | bytes 28
  712.8 103.8 %all-reduce.5.cloned.1.call-start = ((), (), s32[]{:S(2)}) async-start(), calls=%async_computation.3 | async-start | bytes 262144 | tf_op jit(solution)/shard_map/psum | solution.py:169
  817.6 6.3 copy-start.3
Sparse Core Ops, SparseCore 0:
  97.4 82.8 reduce-scatter.2
  217.0 17.4 reduce-scatter.4
  283.5 17.4 reduce-scatter.4
  350.0 17.5 reduce-scatter.4
  416.5 17.4 reduce-scatter.4
  483.1 17.5 reduce-scatter.4
  549.6 17.4 reduce-scatter.4
  616.1 17.4 reduce-scatter.4
  682.6 17.4 reduce-scatter.4
  725.7 90.8 all-reduce.4
where the time goes:
time: 832 us; the launch traced here: 831 us
  waiting for transfers between devices  326 us (39%)
  blocking collectives  204 us (25%)
  matrix products  177 us (21%)
  other arithmetic  50.2 us (6%)
  local copies, waits for them, and re-layouts  43.8 us (5%)
  between operations  16.2 us (2%)
  starting transfers between devices  12.4 us (1%)
    reduce_scatter x8, waiting for transfers between devices, section_block(): lax.psum_scatter(partial_out.astype(jnp.bfloat16), 'tensor', scatter_dime...  141 us
    all_gather x9, blocking collectives, whole_rows(): return lax.all_gather(hidden, 'tensor', axis=1, tiled=True)  96.8 us
    dot_general x8, matrix products, section_block(): projected = jnp.dot(normed, w_in, preferred_element_type=jnp.float32)  83.3 us
    dot_general x8, matrix products, section_block(): partial_out = jnp.dot(mixed, out_proj, preferred_element_type=jnp.float32)  76.2 us
    ppermute x8, waiting for transfers between devices, passed_along(): return lax.ppermute(block, axis, route)  73.6 us
    psum x1, waiting for transfers between devices, shards(): lax.psum(class_total.astype(jnp.bfloat16), ('dp', 'pipe'))  57.9 us
    reduce_scatter x1, waiting for transfers between devices, shards(): lax.psum_scatter(picked.astype(jnp.float32).astype(jnp.bfloat16), ('dp',...  53.5 us
    all_gather x1, blocking collectives, shards(): lax.all_gather(support_tokens, ('dp', 'pipe'), axis=0, tiled=True)  33 us
  transfers between devices with their start and end apart: 18, of which 18 were waited for; matrix products, arithmetic and copies ran while one was open for 2% of the time, Pallas kernels for 0%

commit v1 on v0

--- a/solution.py
+++ b/solution.py
@@ -166,7 +166,9 @@
     class_total = jnp.dot(onehot.T, support_pooled, precision=lax.Precision.HIGHEST)
     class_count = jnp.sum(onehot, axis=0)
     class_total, class_count = (
-        lax.psum(class_total.astype(jnp.bfloat16), ("dp", "pipe")).astype(jnp.float32),
+        jnp.sum(lax.all_gather(class_total.astype(jnp.bfloat16), ("dp", "pipe")), axis=0).astype(
+            jnp.float32
+        ),
         lax.psum(class_count.astype(jnp.bfloat16), ("dp", "pipe")).astype(jnp.float32),
     )
     prototypes = class_total / class_count[:, None]

time: 832 us -> 785 us (0.944)
  waiting for transfers between devices: 326 us -> 276 us
    psum x1 -> x0, waiting for transfers between devices: 57.9 us -> none  [shards(): lax.psum(class_total.astype(jnp.bfloat16), ('dp', 'pipe'))]
  transfers between devices with their start and end apart: 18 -> 18, of which waited for: 18 -> 18; matrix products, arithmetic and copies ran while one was open for 2% -> 3% of each run, Pallas kernels for 0% -> 0%
where the time goes in v1:
time: 785 us; the launch traced here: 781 us
  waiting for transfers between devices  276 us (35%)
  blocking collectives  204 us (26%)
  matrix products  177 us (23%)
  other arithmetic  51.3 us (7%)
  local copies, waits for them, and re-layouts  43.8 us (6%)
  between operations  16.2 us (2%)
  starting transfers between devices  12.4 us (2%)
    reduce_scatter x8, waiting for transfers between devices, section_block(): lax.psum_scatter(partial_out.astype(jnp.bfloat16), 'tensor', scatter_dime...  141 us
    all_gather x9, blocking collectives, whole_rows(): return lax.all_gather(hidden, 'tensor', axis=1, tiled=True)  96.8 us
    dot_general x8, matrix products, section_block(): projected = jnp.dot(normed, w_in, preferred_element_type=jnp.float32)  83.3 us
    dot_general x8, matrix products, section_block(): partial_out = jnp.dot(mixed, out_proj, preferred_element_type=jnp.float32)  76.2 us
    ppermute x8, waiting for transfers between devices, passed_along(): return lax.ppermute(block, axis, route)  73.6 us
    reduce_scatter x1, waiting for transfers between devices, shards(): lax.psum_scatter(picked.astype(jnp.float32).astype(jnp.bfloat16), ('dp',...  53.5 us
    all_gather x1, blocking collectives, shards(): lax.all_gather(support_tokens, ('dp', 'pipe'), axis=0, tiled=True)  33 us
    psum x1, blocking collectives, shards(): lax.psum(class_count.astype(jnp.bfloat16), ('dp', 'pipe'))  32.5 us
  transfers between devices with their start and end apart: 18, of which 18 were waited for; matrix products, arithmetic and copies ran while one was open for 3% of the time, Pallas kernels for 0%

profile of v1, /device:TPU:8, one launch (start us, length us, event | category | flops | bytes accessed | tf_op | source)
XLA Modules:
  0.0 781.3 jit_solution(18366740458328289629)
XLA Ops:
  7.2 29.0 %all-gather.2 = s32[16,1,32]{2,1,0:T(1,128)S(1)} all-gather(s32[1,1,32]{2,1,0:T(1,128)} %bitcast.119), channel_id=1, replica_groups=mesh['dp'=4,'pipe'=4,'tensor'=2] {'dp','pipe'}, dimensions={0}, use_global_device_ids=true | all-gather | bytes 2176 | tf_op jit(solution)/shard_map/all_gather | solution.py:72
  36.2 33.0 %all-gather.1 = s32[16,2,32]{2,1,0:T(2,128)S(1)} all-gather(s32[1,2,32]{2,1,0:T(2,128)} %bitcast.115), channel_id=1, replica_groups=mesh['dp'=4,'pipe'=4,'tensor'=2] {'dp','pipe'}, dimensions={0}, use_global_device_ids=true | all-gather | bytes 4352 | tf_op jit(solution)/shard_map/all_gather | solution.py:71
  69.7 20.5 %gather_fusion = bf16[1536,2048]{1,0:T(8,128)(2,1)} fusion(bf16[4008,2048]{1,0:T(8,128)(2,1)} %param.21, s32[2048]{0:T(1024)S(1)} %pad_clamp_fusion), kind=kCustom, calls=%fused_computation | custom fusion | bytes 12589056 | tf_op jit(solution)/shard_map/jit(_take)/gather | solution.py:81
  108.2 18.7 %pad_maximum_fusion = bf16[4096,3072]{1,0:T(8,128)(2,1)} fusion(bf16[4096,512]{1,0:T(8,128)(2,1)} %bitcast.105, bf16[4096,512]{1,0:T(8,128)(2,1)} %bitcast.106, bf16[4096,2048]{1,0:T(8,128)(2,1)} %bitcast.100), kind=kLoop, calls=%fused_computation.54 | loop fusion | flops 75497472 | bytes 50331648 | tf_op jit(solution)/shard_map/concatenate | solution.py:98
  126.8 53.5 %reduce-scatter.3.cloned.1.call-done = bf16[96,2048]{1,0:T(8,128)(2,1)} async-done(((bf16[1536,2048]{1,0:T(8,128)(2,1)}), bf16[96,2048]{1,0:T(8,128)(2,1)}) %reduce-scatter.3.cloned.1.call-update) | async-done | bytes 393232 | tf_op jit(solution)/shard_map/reduce_scatter | solution.py:83
  180.3 532.5 %while.16 = (s32[]{:T(128)}, bf16[96,2048]{1,0:T(8,128)(2,1)}, s32[]{:T(128)}, f32[1,4096]{1,0:T(1,128)S(1)}, bf16[4096,3072]{1,0:T(8,128)(2,1)}, /*index=5*/s32...) while((s32[]{:T(128)}, bf16[96,2048]{1,0:T(8,128)(2,1)}, ...), condition=%wide.region_6.7_spmd.clone, body=%wide.region_1.0_spmd.clone.sunk | while | flops 4072005120 | bytes 66611072 | solution.py:152
  180.4 11.0 %all_gather.40 = bf16[96,4096]{1,0:T(8,128)(2,1)S(1)} all-gather(bf16[96,2048]{1,0:T(8,128)(2,1)} %get-tuple-element.408), channel_id=1, replica_groups=mesh['dp'=4,'pipe'=4,'tensor'=2] {'tensor'}, dimensions={1}, use_global_device_ids=true | all-gather | bytes 1179648 | tf_op jit(solution)/shard_map/while/body/eval_jaxpr/all_gather | solution.py:38
  191.6 10.4 %fusion.89 = f32[96,3072]{1,0:T(8,128)S(1)} fusion(bf16[4096,3072]{1,0:T(8,128)(2,1)} %get-tuple-element.427, bf16[96,4096]{1,0:T(8,128)(2,1)S(1)} %all_gather.40, f32[4096]{0:T(1024)S(1)} %bitcast.110, f32[96]{0:T(128)S(1)} %add_rsqrt_fusion.3), kind=kOutput, calls=%fused_computation.17.clone.1 | convolution fusion | flops 2417491968 | bytes 27148672 | tf_op jit(solution)/shard_map/while/body/eval_jaxpr/dot_general | solution.py:106
  207.3 9.5 %convolution_convert_fusion.4 = bf16[96,4096]{1,0:T(8,128)(2,1)} fusion(bf16[96,2048]{1,0:T(8,128)(2,1)S(1)} %reshape.355, bf16[2048,4096]{1,0:T(8,128)(2,1)} %get-tuple-element.431), kind=kOutput, calls=%fused_computation.4.clone.1 | convolution fusion | flops 1611005952 | bytes 17956864 | tf_op jit(solution)/shard_map/while/body/eval_jaxpr/dot_general | solution.py:132
  216.9 17.6 %reduce-scatter.5.cloned.1.call-done = bf16[96,2048]{1,0:T(8,128)(2,1)} async-done(((bf16[96,4096]{1,0:T(8,128)(2,1)}), bf16[96,2048]{1,0:T(8,128)(2,1)}) %reduce-scatter.5.cloned.1.call-update) | async-done | bytes 393232 | tf_op jit(solution)/shard_map/while/body/eval_jaxpr/reduce_scatter | solution.py:133
  237.1 9.2 %collective-permute-done = bf16[96,2048]{1,0:T(8,128)(2,1)S(1)} collective-permute-done((bf16[96,2048]{1,0:T(8,128)(2,1)S(1)}, bf16[96,2048]{1,0:T(8,128)(2,1)S(1)}, u32[]{:S(2)}, u32[]{:S(2)}) %collective-permute-start) | collective-permute-done | bytes 393248 | tf_op jit(solution)/shard_map/while/body/eval_jaxpr/ppermute | solution.py:18
  247.2 10.7 %all_gather.40 = bf16[96,4096]{1,0:T(8,128)(2,1)S(1)} all-gather(bf16[96,2048]{1,0:T(8,128)(2,1)} %get-tuple-element.408), channel_id=1, replica_groups=mesh['dp'=4,'pipe'=4,'tensor'=2] {'tensor'}, dimensions={1}, use_global_device_ids=true | all-gather | bytes 1179648 | tf_op jit(solution)/shard_map/while/body/eval_jaxpr/all_gather | solution.py:38
  258.1 10.4 %fusion.89 = f32[96,3072]{1,0:T(8,128)S(1)} fusion(bf16[4096,3072]{1,0:T(8,128)(2,1)} %get-tuple-element.427, bf16[96,4096]{1,0:T(8,128)(2,1)S(1)} %all_gather.40, f32[4096]{0:T(1024)S(1)} %bitcast.110, f32[96]{0:T(128)S(1)} %add_rsqrt_fusion.3), kind=kOutput, calls=%fused_computation.17.clone.1 | convolution fusion | flops 2417491968 | bytes 27148672 | tf_op jit(solution)/shard_map/while/body/eval_jaxpr/dot_general | solution.py:106
  273.8 9.5 %convolution_convert_fusion.4 = bf16[96,4096]{1,0:T(8,128)(2,1)} fusion(bf16[96,2048]{1,0:T(8,128)(2,1)S(1)} %reshape.355, bf16[2048,4096]{1,0:T(8,128)(2,1)} %get-tuple-element.431), kind=kOutput, calls=%fused_computation.4.clone.1 | convolution fusion | flops 1611005952 | bytes 17956864 | tf_op jit(solution)/shard_map/while/body/eval_jaxpr/dot_general | solution.py:132
  283.4 17.6 %reduce-scatter.5.cloned.1.call-done = bf16[96,2048]{1,0:T(8,128)(2,1)} async-done(((bf16[96,4096]{1,0:T(8,128)(2,1)}), bf16[96,2048]{1,0:T(8,128)(2,1)}) %reduce-scatter.5.cloned.1.call-update) | async-done | bytes 393232 | tf_op jit(solution)/shard_map/while/body/eval_jaxpr/reduce_scatter | solution.py:133
  303.7 9.2 %collective-permute-done = bf16[96,2048]{1,0:T(8,128)(2,1)S(1)} collective-permute-done((bf16[96,2048]{1,0:T(8,128)(2,1)S(1)}, bf16[96,2048]{1,0:T(8,128)(2,1)S(1)}, u32[]{:S(2)}, u32[]{:S(2)}) %collective-permute-start) | collective-permute-done | bytes 393248 | tf_op jit(solution)/shard_map/while/body/eval_jaxpr/ppermute | solution.py:18
  313.7 10.7 %all_gather.40 = bf16[96,4096]{1,0:T(8,128)(2,1)S(1)} all-gather(bf16[96,2048]{1,0:T(8,128)(2,1)} %get-tuple-element.408), channel_id=1, replica_groups=mesh['dp'=4,'pipe'=4,'tensor'=2] {'tensor'}, dimensions={1}, use_global_device_ids=true | all-gather | bytes 1179648 | tf_op jit(solution)/shard_map/while/body/eval_jaxpr/all_gather | solution.py:38
  324.6 10.4 %fusion.89 = f32[96,3072]{1,0:T(8,128)S(1)} fusion(bf16[4096,3072]{1,0:T(8,128)(2,1)} %get-tuple-element.427, bf16[96,4096]{1,0:T(8,128)(2,1)S(1)} %all_gather.40, f32[4096]{0:T(1024)S(1)} %bitcast.110, f32[96]{0:T(128)S(1)} %add_rsqrt_fusion.3), kind=kOutput, calls=%fused_computation.17.clone.1 | convolution fusion | flops 2417491968 | bytes 27148672 | tf_op jit(solution)/shard_map/while/body/eval_jaxpr/dot_general | solution.py:106
  340.3 9.5 %convolution_convert_fusion.4 = bf16[96,4096]{1,0:T(8,128)(2,1)} fusion(bf16[96,2048]{1,0:T(8,128)(2,1)S(1)} %reshape.355, bf16[2048,4096]{1,0:T(8,128)(2,1)} %get-tuple-element.431), kind=kOutput, calls=%fused_computation.4.clone.1 | convolution fusion | flops 1611005952 | bytes 17956864 | tf_op jit(solution)/shard_map/while/body/eval_jaxpr/dot_general | solution.py:132
  349.9 17.7 %reduce-scatter.5.cloned.1.call-done = bf16[96,2048]{1,0:T(8,128)(2,1)} async-done(((bf16[96,4096]{1,0:T(8,128)(2,1)}), bf16[96,2048]{1,0:T(8,128)(2,1)}) %reduce-scatter.5.cloned.1.call-update) | async-done | bytes 393232 | tf_op jit(solution)/shard_map/while/body/eval_jaxpr/reduce_scatter | solution.py:133
  370.2 9.2 %collective-permute-done = bf16[96,2048]{1,0:T(8,128)(2,1)S(1)} collective-permute-done((bf16[96,2048]{1,0:T(8,128)(2,1)S(1)}, bf16[96,2048]{1,0:T(8,128)(2,1)S(1)}, u32[]{:S(2)}, u32[]{:S(2)}) %collective-permute-start) | collective-permute-done | bytes 393248 | tf_op jit(solution)/shard_map/while/body/eval_jaxpr/ppermute | solution.py:18
  380.2 10.7 %all_gather.40 = bf16[96,4096]{1,0:T(8,128)(2,1)S(1)} all-gather(bf16[96,2048]{1,0:T(8,128)(2,1)} %get-tuple-element.408), channel_id=1, replica_groups=mesh['dp'=4,'pipe'=4,'tensor'=2] {'tensor'}, dimensions={1}, use_global_device_ids=true | all-gather | bytes 1179648 | tf_op jit(solution)/shard_map/while/body/eval_jaxpr/all_gather | solution.py:38
  391.2 10.4 %fusion.89 = f32[96,3072]{1,0:T(8,128)S(1)} fusion(bf16[4096,3072]{1,0:T(8,128)(2,1)} %get-tuple-element.427, bf16[96,4096]{1,0:T(8,128)(2,1)S(1)} %all_gather.40, f32[4096]{0:T(1024)S(1)} %bitcast.110, f32[96]{0:T(128)S(1)} %add_rsqrt_fusion.3), kind=kOutput, calls=%fused_computation.17.clone.1 | convolution fusion | flops 2417491968 | bytes 27148672 | tf_op jit(solution)/shard_map/while/body/eval_jaxpr/dot_general | solution.py:106
  406.8 9.5 %convolution_convert_fusion.4 = bf16[96,4096]{1,0:T(8,128)(2,1)} fusion(bf16[96,2048]{1,0:T(8,128)(2,1)S(1)} %reshape.355, bf16[2048,4096]{1,0:T(8,128)(2,1)} %get-tuple-element.431), kind=kOutput, calls=%fused_computation.4.clone.1 | convolution fusion | flops 1611005952 | bytes 17956864 | tf_op jit(solution)/shard_map/while/body/eval_jaxpr/dot_general | solution.py:132
  416.4 17.6 %reduce-scatter.5.cloned.1.call-done = bf16[96,2048]{1,0:T(8,128)(2,1)} async-done(((bf16[96,4096]{1,0:T(8,128)(2,1)}), bf16[96,2048]{1,0:T(8,128)(2,1)}) %reduce-scatter.5.cloned.1.call-update) | async-done | bytes 393232 | tf_op jit(solution)/shard_map/while/body/eval_jaxpr/reduce_scatter | solution.py:133
  436.7 9.2 %collective-permute-done = bf16[96,2048]{1,0:T(8,128)(2,1)S(1)} collective-permute-done((bf16[96,2048]{1,0:T(8,128)(2,1)S(1)}, bf16[96,2048]{1,0:T(8,128)(2,1)S(1)}, u32[]{:S(2)}, u32[]{:S(2)}) %collective-permute-start) | collective-permute-done | bytes 393248 | tf_op jit(solution)/shard_map/while/body/eval_jaxpr/ppermute | solution.py:18
  446.7 10.7 %all_gather.40 = bf16[96,4096]{1,0:T(8,128)(2,1)S(1)} all-gather(bf16[96,2048]{1,0:T(8,128)(2,1)} %get-tuple-element.408), channel_id=1, replica_groups=mesh['dp'=4,'pipe'=4,'tensor'=2] {'tensor'}, dimensions={1}, use_global_device_ids=true | all-gather | bytes 1179648 | tf_op jit(solution)/shard_map/while/body/eval_jaxpr/all_gather | solution.py:38
  457.7 10.4 %fusion.89 = f32[96,3072]{1,0:T(8,128)S(1)} fusion(bf16[4096,3072]{1,0:T(8,128)(2,1)} %get-tuple-element.427, bf16[96,4096]{1,0:T(8,128)(2,1)S(1)} %all_gather.40, f32[4096]{0:T(1024)S(1)} %bitcast.110, f32[96]{0:T(128)S(1)} %add_rsqrt_fusion.3), kind=kOutput, calls=%fused_computation.17.clone.1 | convolution fusion | flops 2417491968 | bytes 27148672 | tf_op jit(solution)/shard_map/while/body/eval_jaxpr/dot_general | solution.py:106
  473.4 9.5 %convolution_convert_fusion.4 = bf16[96,4096]{1,0:T(8,128)(2,1)} fusion(bf16[96,2048]{1,0:T(8,128)(2,1)S(1)} %reshape.355, bf16[2048,4096]{1,0:T(8,128)(2,1)} %get-tuple-element.431), kind=kOutput, calls=%fused_computation.4.clone.1 | convolution fusion | flops 1611005952 | bytes 17956864 | tf_op jit(solution)/shard_map/while/body/eval_jaxpr/dot_general | solution.py:132
  483.0 17.6 %reduce-scatter.5.cloned.1.call-done = bf16[96,2048]{1,0:T(8,128)(2,1)} async-done(((bf16[96,4096]{1,0:T(8,128)(2,1)}), bf16[96,2048]{1,0:T(8,128)(2,1)}) %reduce-scatter.5.cloned.1.call-update) | async-done | bytes 393232 | tf_op jit(solution)/shard_map/while/body/eval_jaxpr/reduce_scatter | solution.py:133
  503.3 9.2 %collective-permute-done = bf16[96,2048]{1,0:T(8,128)(2,1)S(1)} collective-permute-done((bf16[96,2048]{1,0:T(8,128)(2,1)S(1)}, bf16[96,2048]{1,0:T(8,128)(2,1)S(1)}, u32[]{:S(2)}, u32[]{:S(2)}) %collective-permute-start) | collective-permute-done | bytes 393248 | tf_op jit(solution)/shard_map/while/body/eval_jaxpr/ppermute | solution.py:18
  513.3 10.7 %all_gather.40 = bf16[96,4096]{1,0:T(8,128)(2,1)S(1)} all-gather(bf16[96,2048]{1,0:T(8,128)(2,1)} %get-tuple-element.408), channel_id=1, replica_groups=mesh['dp'=4,'pipe'=4,'tensor'=2] {'tensor'}, dimensions={1}, use_global_device_ids=true | all-gather | bytes 1179648 | tf_op jit(solution)/shard_map/while/body/eval_jaxpr/all_gather | solution.py:38
  524.2 10.4 %fusion.89 = f32[96,3072]{1,0:T(8,128)S(1)} fusion(bf16[4096,3072]{1,0:T(8,128)(2,1)} %get-tuple-element.427, bf16[96,4096]{1,0:T(8,128)(2,1)S(1)} %all_gather.40, f32[4096]{0:T(1024)S(1)} %bitcast.110, f32[96]{0:T(128)S(1)} %add_rsqrt_fusion.3), kind=kOutput, calls=%fused_computation.17.clone.1 | convolution fusion | flops 2417491968 | bytes 27148672 | tf_op jit(solution)/shard_map/while/body/eval_jaxpr/dot_general | solution.py:106
  539.9 9.5 %convolution_convert_fusion.4 = bf16[96,4096]{1,0:T(8,128)(2,1)} fusion(bf16[96,2048]{1,0:T(8,128)(2,1)S(1)} %reshape.355, bf16[2048,4096]{1,0:T(8,128)(2,1)} %get-tuple-element.431), kind=kOutput, calls=%fused_computation.4.clone.1 | convolution fusion | flops 1611005952 | bytes 17956864 | tf_op jit(solution)/shard_map/while/body/eval_jaxpr/dot_general | solution.py:132
  549.5 17.6 %reduce-scatter.5.cloned.1.call-done = bf16[96,2048]{1,0:T(8,128)(2,1)} async-done(((bf16[96,4096]{1,0:T(8,128)(2,1)}), bf16[96,2048]{1,0:T(8,128)(2,1)}) %reduce-scatter.5.cloned.1.call-update) | async-done | bytes 393232 | tf_op jit(solution)/shard_map/while/body/eval_jaxpr/reduce_scatter | solution.py:133
  569.8 9.2 %collective-permute-done = bf16[96,2048]{1,0:T(8,128)(2,1)S(1)} collective-permute-done((bf16[96,2048]{1,0:T(8,128)(2,1)S(1)}, bf16[96,2048]{1,0:T(8,128)(2,1)S(1)}, u32[]{:S(2)}, u32[]{:S(2)}) %collective-permute-start) | collective-permute-done | bytes 393248 | tf_op jit(solution)/shard_map/while/body/eval_jaxpr/ppermute | solution.py:18
  579.8 10.7 %all_gather.40 = bf16[96,4096]{1,0:T(8,128)(2,1)S(1)} all-gather(bf16[96,2048]{1,0:T(8,128)(2,1)} %get-tuple-element.408), channel_id=1, replica_groups=mesh['dp'=4,'pipe'=4,'tensor'=2] {'tensor'}, dimensions={1}, use_global_device_ids=true | all-gather | bytes 1179648 | tf_op jit(solution)/shard_map/while/body/eval_jaxpr/all_gather | solution.py:38
  590.8 10.4 %fusion.89 = f32[96,3072]{1,0:T(8,128)S(1)} fusion(bf16[4096,3072]{1,0:T(8,128)(2,1)} %get-tuple-element.427, bf16[96,4096]{1,0:T(8,128)(2,1)S(1)} %all_gather.40, f32[4096]{0:T(1024)S(1)} %bitcast.110, f32[96]{0:T(128)S(1)} %add_rsqrt_fusion.3), kind=kOutput, calls=%fused_computation.17.clone.1 | convolution fusion | flops 2417491968 | bytes 27148672 | tf_op jit(solution)/shard_map/while/body/eval_jaxpr/dot_general | solution.py:106
  606.5 9.5 %convolution_convert_fusion.4 = bf16[96,4096]{1,0:T(8,128)(2,1)} fusion(bf16[96,2048]{1,0:T(8,128)(2,1)S(1)} %reshape.355, bf16[2048,4096]{1,0:T(8,128)(2,1)} %get-tuple-element.431), kind=kOutput, calls=%fused_computation.4.clone.1 | convolution fusion | flops 1611005952 | bytes 17956864 | tf_op jit(solution)/shard_map/while/body/eval_jaxpr/dot_general | solution.py:132
  616.0 17.6 %reduce-scatter.5.cloned.1.call-done = bf16[96,2048]{1,0:T(8,128)(2,1)} async-done(((bf16[96,4096]{1,0:T(8,128)(2,1)}), bf16[96,2048]{1,0:T(8,128)(2,1)}) %reduce-scatter.5.cloned.1.call-update) | async-done | bytes 393232 | tf_op jit(solution)/shard_map/while/body/eval_jaxpr/reduce_scatter | solution.py:133
  636.3 9.2 %collective-permute-done = bf16[96,2048]{1,0:T(8,128)(2,1)S(1)} collective-permute-done((bf16[96,2048]{1,0:T(8,128)(2,1)S(1)}, bf16[96,2048]{1,0:T(8,128)(2,1)S(1)}, u32[]{:S(2)}, u32[]{:S(2)}) %collective-permute-start) | collective-permute-done | bytes 393248 | tf_op jit(solution)/shard_map/while/body/eval_jaxpr/ppermute | solution.py:18
  646.3 10.7 %all_gather.40 = bf16[96,4096]{1,0:T(8,128)(2,1)S(1)} all-gather(bf16[96,2048]{1,0:T(8,128)(2,1)} %get-tuple-element.408), channel_id=1, replica_groups=mesh['dp'=4,'pipe'=4,'tensor'=2] {'tensor'}, dimensions={1}, use_global_device_ids=true | all-gather | bytes 1179648 | tf_op jit(solution)/shard_map/while/body/eval_jaxpr/all_gather | solution.py:38
  657.3 10.4 %fusion.89 = f32[96,3072]{1,0:T(8,128)S(1)} fusion(bf16[4096,3072]{1,0:T(8,128)(2,1)} %get-tuple-element.427, bf16[96,4096]{1,0:T(8,128)(2,1)S(1)} %all_gather.40, f32[4096]{0:T(1024)S(1)} %bitcast.110, f32[96]{0:T(128)S(1)} %add_rsqrt_fusion.3), kind=kOutput, calls=%fused_computation.17.clone.1 | convolution fusion | flops 2417491968 | bytes 27148672 | tf_op jit(solution)/shard_map/while/body/eval_jaxpr/dot_general | solution.py:106
  673.0 9.5 %convolution_convert_fusion.4 = bf16[96,4096]{1,0:T(8,128)(2,1)} fusion(bf16[96,2048]{1,0:T(8,128)(2,1)S(1)} %reshape.355, bf16[2048,4096]{1,0:T(8,128)(2,1)} %get-tuple-element.431), kind=kOutput, calls=%fused_computation.4.clone.1 | convolution fusion | flops 1611005952 | bytes 17956864 | tf_op jit(solution)/shard_map/while/body/eval_jaxpr/dot_general | solution.py:132
  682.5 17.6 %reduce-scatter.5.cloned.1.call-done = bf16[96,2048]{1,0:T(8,128)(2,1)} async-done(((bf16[96,4096]{1,0:T(8,128)(2,1)}), bf16[96,2048]{1,0:T(8,128)(2,1)}) %reduce-scatter.5.cloned.1.call-update) | async-done | bytes 393232 | tf_op jit(solution)/shard_map/while/body/eval_jaxpr/reduce_scatter | solution.py:133
  702.8 9.2 %collective-permute-done = bf16[96,2048]{1,0:T(8,128)(2,1)S(1)} collective-permute-done((bf16[96,2048]{1,0:T(8,128)(2,1)S(1)}, bf16[96,2048]{1,0:T(8,128)(2,1)S(1)}, u32[]{:S(2)}, u32[]{:S(2)}) %collective-permute-start) | collective-permute-done | bytes 393248 | tf_op jit(solution)/shard_map/while/body/eval_jaxpr/ppermute | solution.py:18
  712.8 10.8 %all_gather.35 = bf16[96,4096]{1,0:T(8,128)(2,1)S(1)} all-gather(bf16[96,2048]{1,0:T(8,128)(2,1)} %get-tuple-element.268), channel_id=1, replica_groups=mesh['dp'=4,'pipe'=4,'tensor'=2] {'tensor'}, dimensions={1}, use_global_device_ids=true | all-gather | bytes 1179648 | tf_op jit(solution)/shard_map/all_gather | solution.py:38
  725.6 32.5 %psum.14 = bf16[32]{0:T(256)(128)(2,1)S(1)} all-reduce(bf16[32]{0:T(256)(128)(2,1)S(1)} %convert_reduce_fusion), channel_id=1, replica_groups=mesh['dp'=4,'pipe'=4,'tensor'=2] {'dp','pipe'}, use_global_device_ids=true, to_apply=%region_11.12 | all-reduce | flops 32 | bytes 128 | tf_op jit(solution)/shard_map/psum | solution.py:172
  (315 shorter events, 105.6 us)
Async XLA Ops:
  7.2 173.2 %reduce-scatter.3.cloned.1.call-start = ((), (), s32[]{:S(2)}) async-start(), calls=%async_computation.2 | async-start | bytes 6684672 | tf_op jit(solution)/shard_map/reduce_scatter | solution.py:83
  97.3 0.7 copy-start.6
  97.3 2.1 copy-start.5
  108.2 72.1 %copy-start.2 = (f32[1,4096]{1,0:T(1,128)S(1)}, f32[1,4096]{1,0:T(1,128)}, u32[]{:S(2)}) copy-start(f32[1,4096]{1,0:T(1,128)} %param.22) | copy-start | bytes 49156
  180.3 543.7 %dynamic-slice-start = ((f32[4096]{0:T(1024)}, s32[]{:T(128)}), f32[2048]{0:T(1024)S(1)}, s32[]{:S(2)}) async-start(f32[4096]{0:T(1024)} %param.27, s32[]{:T(128)} %select_n.115), calls=%async_computation.5 | async-start | bytes 16896 | tf_op jit(solution)/shard_map/dynamic_slice | solution.py:153
  180.3 54.2 %reduce-scatter.5.cloned.1.call-start = ((), (), s32[]{:S(2)}) async-start(), calls=%async_computation.4 | async-start | bytes 1179648 | tf_op jit(solution)/shard_map/while/body/eval_jaxpr/reduce_scatter | solution.py:133
  207.3 27.2 %copy-start = (bf16[96,2048]{1,0:T(8,128)(2,1)S(1)}, bf16[96,2048]{1,0:T(8,128)(2,1)}, u32[]{:S(2)}) copy-start(bf16[96,2048]{1,0:T(8,128)(2,1)} %get-tuple-element.408) | copy-start | bytes 1179652 | tf_op jit(solution)/shard_map/while
  235.6 10.8 %collective-permute-start = (bf16[96,2048]{1,0:T(8,128)(2,1)S(1)}, bf16[96,2048]{1,0:T(8,128)(2,1)S(1)}, u32[]{:S(2)}, u32[]{:S(2)}) collective-permute-start(bf16[96,2048]{1,0:T(8,128)(2,1)S(1)} %fusion.94), channel_id=1, source_target_pairs={{6,0},{0,2},{2,4},{4,6},{7,1},{1,3},{3,5},{5,7},{14,8},{8,10},{10,... | collective-permute-start | bytes 1179656 | tf_op jit(solution)/shard_map/while/body/eval_jaxpr/ppermute | solution.py:18
  246.4 0.8 copy-start.1
  247.1 53.9 %reduce-scatter.5.cloned.1.call-start = ((), (), s32[]{:S(2)}) async-start(), calls=%async_computation.4 | async-start | bytes 1179648 | tf_op jit(solution)/shard_map/while/body/eval_jaxpr/reduce_scatter | solution.py:133
  273.8 27.2 %copy-start = (bf16[96,2048]{1,0:T(8,128)(2,1)S(1)}, bf16[96,2048]{1,0:T(8,128)(2,1)}, u32[]{:S(2)}) copy-start(bf16[96,2048]{1,0:T(8,128)(2,1)} %get-tuple-element.408) | copy-start | bytes 1179652 | tf_op jit(solution)/shard_map/while
  302.1 10.7 %collective-permute-start = (bf16[96,2048]{1,0:T(8,128)(2,1)S(1)}, bf16[96,2048]{1,0:T(8,128)(2,1)S(1)}, u32[]{:S(2)}, u32[]{:S(2)}) collective-permute-start(bf16[96,2048]{1,0:T(8,128)(2,1)S(1)} %fusion.94), channel_id=1, source_target_pairs={{6,0},{0,2},{2,4},{4,6},{7,1},{1,3},{3,5},{5,7},{14,8},{8,10},{10,... | collective-permute-start | bytes 1179656 | tf_op jit(solution)/shard_map/while/body/eval_jaxpr/ppermute | solution.py:18
  312.9 0.8 copy-start.1
  313.6 53.9 %reduce-scatter.5.cloned.1.call-start = ((), (), s32[]{:S(2)}) async-start(), calls=%async_computation.4 | async-start | bytes 1179648 | tf_op jit(solution)/shard_map/while/body/eval_jaxpr/reduce_scatter | solution.py:133
  340.3 27.3 %copy-start = (bf16[96,2048]{1,0:T(8,128)(2,1)S(1)}, bf16[96,2048]{1,0:T(8,128)(2,1)}, u32[]{:S(2)}) copy-start(bf16[96,2048]{1,0:T(8,128)(2,1)} %get-tuple-element.408) | copy-start | bytes 1179652 | tf_op jit(solution)/shard_map/while
  368.7 10.7 %collective-permute-start = (bf16[96,2048]{1,0:T(8,128)(2,1)S(1)}, bf16[96,2048]{1,0:T(8,128)(2,1)S(1)}, u32[]{:S(2)}, u32[]{:S(2)}) collective-permute-start(bf16[96,2048]{1,0:T(8,128)(2,1)S(1)} %fusion.94), channel_id=1, source_target_pairs={{6,0},{0,2},{2,4},{4,6},{7,1},{1,3},{3,5},{5,7},{14,8},{8,10},{10,... | collective-permute-start | bytes 1179656 | tf_op jit(solution)/shard_map/while/body/eval_jaxpr/ppermute | solution.py:18
  379.4 0.8 copy-start.1
  380.2 53.9 %reduce-scatter.5.cloned.1.call-start = ((), (), s32[]{:S(2)}) async-start(), calls=%async_computation.4 | async-start | bytes 1179648 | tf_op jit(solution)/shard_map/while/body/eval_jaxpr/reduce_scatter | solution.py:133
  406.8 27.2 %copy-start = (bf16[96,2048]{1,0:T(8,128)(2,1)S(1)}, bf16[96,2048]{1,0:T(8,128)(2,1)}, u32[]{:S(2)}) copy-start(bf16[96,2048]{1,0:T(8,128)(2,1)} %get-tuple-element.408) | copy-start | bytes 1179652 | tf_op jit(solution)/shard_map/while
  435.2 10.8 %collective-permute-start = (bf16[96,2048]{1,0:T(8,128)(2,1)S(1)}, bf16[96,2048]{1,0:T(8,128)(2,1)S(1)}, u32[]{:S(2)}, u32[]{:S(2)}) collective-permute-start(bf16[96,2048]{1,0:T(8,128)(2,1)S(1)} %fusion.94), channel_id=1, source_target_pairs={{6,0},{0,2},{2,4},{4,6},{7,1},{1,3},{3,5},{5,7},{14,8},{8,10},{10,... | collective-permute-start | bytes 1179656 | tf_op jit(solution)/shard_map/while/body/eval_jaxpr/ppermute | solution.py:18
  445.9 0.8 copy-start.1
  446.7 53.9 %reduce-scatter.5.cloned.1.call-start = ((), (), s32[]{:S(2)}) async-start(), calls=%async_computation.4 | async-start | bytes 1179648 | tf_op jit(solution)/shard_map/while/body/eval_jaxpr/reduce_scatter | solution.py:133
  473.4 27.2 %copy-start = (bf16[96,2048]{1,0:T(8,128)(2,1)S(1)}, bf16[96,2048]{1,0:T(8,128)(2,1)}, u32[]{:S(2)}) copy-start(bf16[96,2048]{1,0:T(8,128)(2,1)} %get-tuple-element.408) | copy-start | bytes 1179652 | tf_op jit(solution)/shard_map/while
  501.7 10.7 %collective-permute-start = (bf16[96,2048]{1,0:T(8,128)(2,1)S(1)}, bf16[96,2048]{1,0:T(8,128)(2,1)S(1)}, u32[]{:S(2)}, u32[]{:S(2)}) collective-permute-start(bf16[96,2048]{1,0:T(8,128)(2,1)S(1)} %fusion.94), channel_id=1, source_target_pairs={{6,0},{0,2},{2,4},{4,6},{7,1},{1,3},{3,5},{5,7},{14,8},{8,10},{10,... | collective-permute-start | bytes 1179656 | tf_op jit(solution)/shard_map/while/body/eval_jaxpr/ppermute | solution.py:18
  512.5 0.8 copy-start.1
  513.2 53.9 %reduce-scatter.5.cloned.1.call-start = ((), (), s32[]{:S(2)}) async-start(), calls=%async_computation.4 | async-start | bytes 1179648 | tf_op jit(solution)/shard_map/while/body/eval_jaxpr/reduce_scatter | solution.py:133
  539.9 27.2 %copy-start = (bf16[96,2048]{1,0:T(8,128)(2,1)S(1)}, bf16[96,2048]{1,0:T(8,128)(2,1)}, u32[]{:S(2)}) copy-start(bf16[96,2048]{1,0:T(8,128)(2,1)} %get-tuple-element.408) | copy-start | bytes 1179652 | tf_op jit(solution)/shard_map/while
  568.2 10.8 %collective-permute-start = (bf16[96,2048]{1,0:T(8,128)(2,1)S(1)}, bf16[96,2048]{1,0:T(8,128)(2,1)S(1)}, u32[]{:S(2)}, u32[]{:S(2)}) collective-permute-start(bf16[96,2048]{1,0:T(8,128)(2,1)S(1)} %fusion.94), channel_id=1, source_target_pairs={{6,0},{0,2},{2,4},{4,6},{7,1},{1,3},{3,5},{5,7},{14,8},{8,10},{10,... | collective-permute-start | bytes 1179656 | tf_op jit(solution)/shard_map/while/body/eval_jaxpr/ppermute | solution.py:18
  579.0 0.8 copy-start.1
  579.8 53.8 %reduce-scatter.5.cloned.1.call-start = ((), (), s32[]{:S(2)}) async-start(), calls=%async_computation.4 | async-start | bytes 1179648 | tf_op jit(solution)/shard_map/while/body/eval_jaxpr/reduce_scatter | solution.py:133
  606.5 27.2 %copy-start = (bf16[96,2048]{1,0:T(8,128)(2,1)S(1)}, bf16[96,2048]{1,0:T(8,128)(2,1)}, u32[]{:S(2)}) copy-start(bf16[96,2048]{1,0:T(8,128)(2,1)} %get-tuple-element.408) | copy-start | bytes 1179652 | tf_op jit(solution)/shard_map/while
  634.8 10.8 %collective-permute-start = (bf16[96,2048]{1,0:T(8,128)(2,1)S(1)}, bf16[96,2048]{1,0:T(8,128)(2,1)S(1)}, u32[]{:S(2)}, u32[]{:S(2)}) collective-permute-start(bf16[96,2048]{1,0:T(8,128)(2,1)S(1)} %fusion.94), channel_id=1, source_target_pairs={{6,0},{0,2},{2,4},{4,6},{7,1},{1,3},{3,5},{5,7},{14,8},{8,10},{10,... | collective-permute-start | bytes 1179656 | tf_op jit(solution)/shard_map/while/body/eval_jaxpr/ppermute | solution.py:18
  645.5 0.8 copy-start.1
  646.3 53.9 %reduce-scatter.5.cloned.1.call-start = ((), (), s32[]{:S(2)}) async-start(), calls=%async_computation.4 | async-start | bytes 1179648 | tf_op jit(solution)/shard_map/while/body/eval_jaxpr/reduce_scatter | solution.py:133
  673.0 27.2 %copy-start = (bf16[96,2048]{1,0:T(8,128)(2,1)S(1)}, bf16[96,2048]{1,0:T(8,128)(2,1)}, u32[]{:S(2)}) copy-start(bf16[96,2048]{1,0:T(8,128)(2,1)} %get-tuple-element.408) | copy-start | bytes 1179652 | tf_op jit(solution)/shard_map/while
  701.3 10.7 %collective-permute-start = (bf16[96,2048]{1,0:T(8,128)(2,1)S(1)}, bf16[96,2048]{1,0:T(8,128)(2,1)S(1)}, u32[]{:S(2)}, u32[]{:S(2)}) collective-permute-start(bf16[96,2048]{1,0:T(8,128)(2,1)S(1)} %fusion.94), channel_id=1, source_target_pairs={{6,0},{0,2},{2,4},{4,6},{7,1},{1,3},{3,5},{5,7},{14,8},{8,10},{10,... | collective-permute-start | bytes 1179656 | tf_op jit(solution)/shard_map/while/body/eval_jaxpr/ppermute | solution.py:18
  712.0 0.8 copy-start.1
  712.8 11.6 %copy-start.4 = (s32[2,1]{0,1:T(1,128)S(1)}, s32[2,1]{0,1:T(1,128)}, u32[]{:S(2)}) copy-start(s32[2,1]{0,1:T(1,128)} %param.17) | copy-start | bytes 28
  712.8 53.3 %all-gather.5.cloned.1.call-start = ((), (), s32[]{:S(2)}) async-start(), calls=%async_computation.3 | async-start | bytes 2228224 | tf_op jit(solution)/shard_map/all_gather | solution.py:169
  768.1 6.3 copy-start.3
Sparse Core Ops, SparseCore 0:
  97.4 82.8 reduce-scatter.2
  217.0 17.4 reduce-scatter.4
  283.5 17.4 reduce-scatter.4
  350.0 17.5 reduce-scatter.4
  416.5 17.4 reduce-scatter.4
  483.1 17.5 reduce-scatter.4
  549.6 17.4 reduce-scatter.4
  616.1 17.4 reduce-scatter.4
  682.6 17.4 reduce-scatter.4
  725.7 40.3 all-gather.4
